TPU v7x, 32 devices: a whole 2x2x4 slice. The times are simulated.
32 devices in a mesh: grp: 2 (over x), seq: 16 (over z, y, core).
Axes of the slice: x: 2, y: 2, z: 4, core: 2. Of those that a mesh axis runs over, the one named last changes fastest.
Arguments:
- cont_query: bfloat16 [64, 32, 2560], P(('grp', 'seq')), parts along dimension 0, may hold values from -180 to 180
- cont_key: bfloat16 [64, 32, 512], P(('grp', 'seq')), parts along dimension 0, may hold values from -6 to 6
- cont_value: bfloat16 [64, 32, 512], P(('grp', 'seq')), parts along dimension 0, may hold values from -6 to 6
- prefix_key: bfloat16 [4, 2048, 512], P('grp', 'seq'), parts along dimension 0, may hold values from -7 to 7
- prefix_value: bfloat16 [4, 2048, 512], P('grp', 'seq'), parts along dimension 0, may hold values from -6 to 6
- out_weight: bfloat16 [2560, 2560], P(None, 'seq'), may hold values from -0.125 to 0.125
- norm_gain: float32 [2560], replicated, may hold values from 0.5 to 1.5
- lm_head: bfloat16 [2560, 76032], P(None, 'seq'), may hold values from -18 to 18
- target_ids: int32 [64, 32], P(('grp', 'seq')), parts along dimension 0, may hold values from 0 to 76031
- cont_len: int32 [64], P(('grp', 'seq')), parts along dimension 0, may hold values from 8 to 32
- prompt_len: int32 [4], P('grp'), parts along dimension 0, may hold values from 1024 to 2048
- group_of: int32 [64], P('grp'), parts along dimension 0, may hold values from 0 to 1, as said below
- rewards: float32 [64], P(('grp', 'seq')), parts along dimension 0, may hold values from -13 to 13
Outputs:
- token_logprob: float32 [64, 32], P(('grp', 'seq')), parts along dimension 0
- advantage: float32 [64], P(('grp', 'seq')), parts along dimension 0
- objective: float32 [64], P(('grp', 'seq')), parts along dimension 0
There are 2 independent parts, one for each index of `grp`. A program takes and returns all parts, laid end to end along the dimension named above; an argument that names none is the same for every part. Nothing has to cross between parts.
Inputs may be any that keep to these rules, and one draw needn't show every extreme that they name: `group_of`: each of the 2 prompts is named by exactly 16 continuations.
All inputs are finite; a program needn't handle non-finite values.
Results may differ from a plain program's by a relative error of at most 0.0026.
Values may be sent and summed in bfloat16 or wider, within the bound.
A program may use at most 128 MiB of HBM per device.

v0:
```python
import functools

import jax
import jax.numpy as jnp
from jax import lax
from jax.experimental import pallas as pl
from jax.experimental.pallas import tpu as pltpu
from jax.sharding import PartitionSpec as P

HD = 128
GROUP = 16
NEGATIVE = -1e30
EPSILON = 1e-06
REWARD_FLOOR = 0.25
MESH = pl.DeviceIdType.MESH
VMEM = pltpu.VMEM
LIMIT = 60 * 1024 * 1024
TILE = 1584
WPARTS = 5
SPLIT = 3
STEP = 32
WIDE = 64
PAIR = 2
QUAD = 4


def pick(table, at):
    out = table[0]
    for i in range(1, len(table)):
        out = jnp.where(at == i, table[i], out)
    return out


class Place:
    def __init__(self, n, planes):
        self.n, self.planes = n, planes
        self.lanes = n // planes
        self.half = self.lanes // 2
        self.me = lax.axis_index("seq")
        self.plane = self.me // self.lanes
        self.lane = self.me % self.lanes
        self.row = self.lane // 2
        self.core = self.lane % 2

    def device(self, plane, row, core):
        return plane * self.lanes + row * 2 + core

    def row_at(self, step):
        return (self.row + step) % self.half

    def sources(self):
        tables = []
        for p in range(self.planes):
            others = [s for s in range(self.planes) if s != p]
            others.sort(key=lambda s: (not self.passes(s, p), abs(s - p)))
            tables.append(others)
        return [
            pick([table[j] for table in tables], self.plane) for j in range(self.planes - 1)
        ]

    def ranked(self, far_first):
        tables = []
        for p in range(self.planes):
            others = [s for s in range(self.planes) if s != p]
            others.sort(key=lambda s: -abs(s - p) if far_first else abs(s - p))
            tables.append(others)
        return [
            pick([table[j] for table in tables], self.plane) for j in range(self.planes - 1)
        ]

    def passes(self, source, p):
        if source < p:
            return p + 1 < self.planes and not (source == 0 and p == 1)
        return p >= 1 and not (source == self.planes - 1 and p == self.planes - 2)


class Wire:
    def __init__(self, send_sem, recv_sem):
        self.send_sem, self.recv_sem = send_sem, recv_sem
        self.sent = []

    def send(self, src, dst, slot, target, when=None):
        copy = pltpu.make_async_remote_copy(
            src_ref=src,
            dst_ref=dst,
            send_sem=self.send_sem.at[len(self.sent)],
            recv_sem=self.recv_sem.at[slot],
            device_id={"seq": target},
            device_id_type=MESH,
        )
        self.sent.append(when)
        if when is None:
            copy.start()
        else:
            pl.when(when())(copy.start)

    def arrived(self, dst, slot, other):
        pltpu.make_async_remote_copy(
            src_ref=dst,
            dst_ref=dst,
            send_sem=self.send_sem.at[0],
            recv_sem=self.recv_sem.at[slot],
            device_id={"seq": other},
            device_id_type=MESH,
        ).wait_recv()

    def drain(self, like, other):
        for i, when in enumerate(self.sent):
            copy = pltpu.make_async_remote_copy(
                src_ref=like,
                dst_ref=like,
                send_sem=self.send_sem.at[i],
                recv_sem=self.recv_sem.at[0],
                device_id={"seq": other},
                device_id_type=MESH,
            )
            if when is None:
                copy.wait_send()
            else:
                pl.when(when())(copy.wait_send)


class Line:
    def __init__(self, at, wire, piece, slot):
        self.at, self.wire, self.piece, self.slot = at, wire, piece, slot

    def peer(self, plane):
        return self.at.device(plane, self.at.row, self.at.core)

    def send_own(self, part):
        at = self.at
        last = at.planes - 1
        mine = self.piece(part, at.plane)
        slot = self.slot(part, at.plane)
        moves = [(1, lambda: at.plane < last), (-1, lambda: at.plane > 0)]
        if at.planes > 2:
            far = jnp.where(at.plane == 0, 2, last - 2)

            def ends():
                return jnp.logical_or(at.plane == 0, at.plane == last)

            self.wire.send(mine, mine, slot, self.peer(far), ends)
        for step, when in moves:
            target = jnp.clip(at.plane + step, 0, last)
            self.wire.send(mine, mine, slot, self.peer(target), when)

    def take(self, part, source):
        at = self.at
        last = at.planes - 1
        got = self.piece(part, source)
        slot = self.slot(part, source)
        self.wire.arrived(got, slot, self.peer(source))
        def toward():
            return jnp.where(source < at.plane, at.plane + 1, at.plane - 1)

        def when():
            target = toward()
            inside = jnp.logical_and(target >= 0, target <= last)
            direct = jnp.logical_or(
                jnp.logical_and(source == 0, at.plane == 1),
                jnp.logical_and(source == last, at.plane == last - 1),
            )
            return jnp.logical_and(inside, jnp.logical_not(direct))

        self.wire.send(got, got, slot, self.peer(jnp.clip(toward(), 0, last)), when)


def layer_kernel(
    n,
    planes,
    group_ref,
    length_ref,
    length_own_ref,
    reward_ref,
    q_ref,
    ck_ref,
    cv_ref,
    pk_ref,
    pv_ref,
    ids_ref,
    w_ref,
    gain_ref,
    head_hbm,
    logprob_out,
    rating_out,
    stats_s,
    meta_s,
    meta_all,
    rating_s,
    q_s,
    ck_s,
    cv_s,
    pk_s,
    pv_s,
    att_s,
    w_s,
    hid_s,
    norm_s,
    factor_s,
    head_s,
    ids_s,
    max_s,
    sum_s,
    pick_s,
    tile_s,
    kv_send,
    kv_recv,
    q_send,
    q_recv,
    p_send,
    p_recv,
    meta_send,
    meta_recv,
    w_send,
    w_recv,
    b_send,
    b_recv,
    c_send,
    c_recv,
    stat_send,
    stat_recv,
    local_sem,
    head_sem,
):
    at = Place(n, planes)
    conts, steps, _ = q_ref.shape
    span = pk_ref.shape[1]
    width = q_ref.shape[2] // planes
    heads = width // HD
    depth = w_ref.shape[1]
    wrows = w_ref.shape[0]
    features = wrows * at.lanes
    vocab = head_hbm.shape[0]
    prompts = pk_ref.shape[0]
    block = PAIR * steps
    halves = planes // PAIR
    subs = conts * halves
    tiles, rest = vocab // TILE, vocab % TILE
    last_row = at.half - 1

    def load(tile, size):
        cut = pl.ds(pl.multiple_of(tile * TILE, 8), size)
        return pltpu.make_async_copy(head_hbm.at[cut], head_s.at[cut], head_sem.at[tile])

    for tile in range(tiles):
        load(tile, TILE).start()
    if rest:
        load(tiles, rest).start()

    lane_of = lax.broadcasted_iota(jnp.int32, (1, 128), 1)
    meta_s[...] = jnp.zeros_like(meta_s)
    for i in range(conts):
        meta_s[0:1, i * steps : (i + 1) * steps] = ids_ref[i : i + 1, :].astype(jnp.float32)
    own_rewards = jnp.zeros((1, 128), jnp.float32)
    for i in range(conts):
        own_rewards = jnp.where(lane_of == i, reward_ref[i], own_rewards)
    meta_s[1:2, :] = own_rewards

    barrier = pltpu.get_barrier_semaphore()
    for d in range(1, n):
        pl.semaphore_signal(
            barrier, inc=1, device_id={"seq": (at.me + d) % n}, device_id_type=MESH
        )
    pl.semaphore_wait(barrier, n - 1)

    locals_ = []

    def local(src, dst):
        copy = pltpu.make_async_copy(src, dst, local_sem.at[len(locals_)])
        copy.start()
        locals_.append(copy)

    sources = at.sources()
    far = at.ranked(True)
    near = at.ranked(False)

    kv = Wire(kv_send, kv_recv)

    def kv_full(part, source):
        start = pl.multiple_of(source * span, 16)
        return (pk_s, pv_s)[part // prompts].at[part % prompts, pl.ds(start, span), :]

    def kv_own(part, plane):
        cut = pl.ds(pl.multiple_of(plane * HD, 128), HD)
        return (pk_ref, pv_ref)[part // prompts].at[part % prompts, :, cut]

    def kv_share(part, source, src, core_only=False):
        slot = part * n + source
        dst = kv_full(part, source)
        if not core_only:
            for e in range(1, at.half):
                kv.send(src, dst, slot, at.device(at.plane, at.row_at(e), at.core))
        kv.send(src, dst, slot, at.device(at.plane, at.row, 1 - at.core))

    ww = Wire(w_send, w_recv)
    wpart = wrows // WPARTS

    def w_full(lane, k):
        start = pl.multiple_of(lane * wrows + k * wpart, 16)
        return w_s.at[pl.ds(start, wpart)]

    def w_core(lane, k):
        piece = w_full(lane, k)
        ww.send(piece, piece, lane * WPARTS + k, at.device(at.plane, at.row, 1 - at.core))

    def w_own(k):
        src = w_ref.at[pl.ds(k * wpart, wpart)]
        slot = at.lane * WPARTS + k
        for e in range(1, at.half):
            ww.send(src, w_full(at.lane, k), slot, at.device(at.plane, at.row_at(e), at.core))
        ww.send(src, w_full(at.lane, k), slot, at.device(at.plane, at.row, 1 - at.core))

    def w_arrived(lane, k):
        other = at.device(at.plane, at.row, 1 - at.core)
        ww.arrived(w_full(lane, k), lane * WPARTS + k, other)

    for part in range(2 * prompts):
        for target in far:
            kv.send(
                kv_own(part, target),
                kv_full(part, at.me),
                part * n + at.me,
                at.device(target, at.row, at.core),
            )
        own = kv_own(part, at.plane)
        kv_share(part, at.me, own)
        local(own, kv_full(part, at.me))
    w_own(0)
    w_own(1)

    meta = Wire(meta_send, meta_recv)
    for d in range(1, n):
        meta.send(meta_s, meta_all.at[at.me], at.me, (at.me + d) % n)
    local(meta_s, meta_all.at[at.me])

    qw = Wire(q_send, q_recv)
    pw = Wire(p_send, p_recv)

    def q_piece(i, source):
        return q_s.at[i, source]

    def c_pieces(i, source):
        return (ck_s.at[i, source], cv_s.at[i, source])

    for i in range(conts):
        for target in far:
            peer = at.device(target, at.row, at.core)
            cut = pl.ds(pl.multiple_of(target * width, 128), width)
            qw.send(q_ref.at[i, :, cut], q_piece(i, at.plane), i * planes + at.plane, peer)
            narrow = pl.ds(pl.multiple_of(target * HD, 128), HD)
            for j, ref in enumerate((ck_ref, cv_ref)):
                pw.send(
                    ref.at[i, :, narrow],
                    c_pieces(i, at.plane)[j],
                    (i * 2 + j) * planes + at.plane,
                    peer,
                )
        own = pl.ds(pl.multiple_of(at.plane * width, 128), width)
        local(q_ref.at[i, :, own], q_piece(i, at.plane))
        narrow = pl.ds(pl.multiple_of(at.plane * HD, 128), HD)
        for j, ref in enumerate((ck_ref, cv_ref)):
            local(ref.at[i, :, narrow], c_pieces(i, at.plane)[j])
    local(w_ref, w_s.at[pl.ds(pl.multiple_of(at.lane * wrows, 16), wrows)])

    max_s[...] = jnp.full_like(max_s, NEGATIVE)
    sum_s[...] = jnp.zeros_like(sum_s)
    pick_s[...] = jnp.zeros_like(pick_s)

    def kv_from_rows(plane, part):
        for e in range(1, at.half):
            source = at.device(plane, at.row_at(e), at.core)
            kv.arrived(kv_full(part, source), part * n + source, source)
            kv_share(part, source, kv_full(part, source), core_only=True)

    def kv_from_plane(plane, part):
        source = at.device(plane, at.row, at.core)
        kv.arrived(kv_full(part, source), part * n + source, source)
        kv_share(part, source, kv_full(part, source))

    for part in range(2 * prompts):
        for plane in near:
            kv_from_plane(plane, part)
        if part == prompts - 1:
            w_own(2)
        if part:
            for plane in [at.plane] + near:
                kv_from_rows(plane, part - 1)
    for k in range(3, WPARTS):
        w_own(k)
    for plane in [at.plane] + near:
        kv_from_rows(plane, 2 * prompts - 1)

    for part in range(2 * prompts):
        for plane in range(planes):
            for row in range(at.half):
                source = at.device(plane, row, 1 - at.core)
                kv.arrived(kv_full(part, source), part * n + source, source)
    for copy in locals_:
        copy.wait()

    def attend(k):
        i, h = k // halves, k % halves
        if h == 0:
            for source in sources:
                peer = at.device(source, at.row, at.core)
                qw.arrived(q_piece(i, source), i * planes + source, peer)
                for j in range(2):
                    pw.arrived(c_pieces(i, source)[j], (i * 2 + j) * planes + source, peer)

        @pl.loop(0, PAIR)
        def _(j):
            plane = h * PAIR + j
            prompt = group_ref[(plane * at.lanes + at.lane) * conts + i]
            length = length_ref[prompt]
            q = q_s[i, plane]
            rows = jnp.concatenate([q[:, h * HD : (h + 1) * HD] for h in range(heads)], axis=0)
            contract = (((1,), (1,)), ((), ()))
            early = lax.dot_general(
                rows, pk_s[prompt], contract, preferred_element_type=jnp.float32
            )
            late = lax.dot_general(
                rows, ck_s[i, plane], contract, preferred_element_type=jnp.float32
            )
            scale = HD ** (-0.5)
            column = lax.broadcasted_iota(jnp.int32, early.shape, 1)
            early = jnp.where(column < length, early * scale, NEGATIVE)
            line = lax.broadcasted_iota(jnp.int32, late.shape, 0) % steps
            late = jnp.where(
                lax.broadcasted_iota(jnp.int32, late.shape, 1) <= line, late * scale, NEGATIVE
            )
            peak = jnp.maximum(
                jnp.max(early, axis=1, keepdims=True), jnp.max(late, axis=1, keepdims=True)
            )
            early = jnp.exp(early - peak).astype(jnp.bfloat16)
            late = jnp.exp(late - peak).astype(jnp.bfloat16)
            total = jnp.sum(early.astype(jnp.float32), axis=1, keepdims=True) + jnp.sum(
                late.astype(jnp.float32), axis=1, keepdims=True
            )
            mixed = jnp.dot(early, pv_s[prompt], preferred_element_type=jnp.float32) + jnp.dot(
                late, cv_s[i, plane], preferred_element_type=jnp.float32
            )
            mixed = (mixed / total).astype(jnp.bfloat16)
            token = pl.ds(pl.multiple_of(j * steps, 16), steps)
            cut = pl.ds(pl.multiple_of(at.plane * width, 128), width)
            att_s[k, token, cut] = jnp.concatenate(
                [mixed[h * steps : (h + 1) * steps] for h in range(heads)], axis=1
            )

    bw = Wire(b_send, b_recv)

    def b_piece(i, plane):
        return att_s.at[i, :, pl.ds(pl.multiple_of(plane * width, 128), width)]

    b_line = Line(at, bw, b_piece, lambda i, plane: i * planes + plane)

    cw = Wire(c_send, c_recv)

    def c_block(i, lane, plane):
        rows = pl.ds(pl.multiple_of(lane * block, 16), block)
        cut = pl.ds(pl.multiple_of(plane * features, 128), features)
        return hid_s.at[i, rows, cut]

    def c_slot(i, lane, plane):
        return i * n + plane * at.lanes + lane

    c_line = Line(
        at,
        cw,
        lambda i, plane: c_block(i, at.lane, plane),
        lambda i, plane: c_slot(i, at.lane, plane),
    )

    def c_core(i, lane, plane):
        piece = c_block(i, lane, plane)
        cw.send(piece, piece, c_slot(i, lane, plane), at.device(at.plane, at.row, 1 - at.core))

    def c_share(i, plane):
        piece = c_block(i, at.lane, plane)
        for e in range(1, at.half):
            cw.send(
                piece,
                piece,
                c_slot(i, at.lane, plane),
                at.device(at.plane, at.row_at(e), at.core),
            )
        c_core(i, at.lane, plane)

    def c_own(i):
        c_line.send_own(i)
        c_share(i, at.plane)

    def c_take(i, plane):
        c_line.take(i, plane)
        c_share(i, plane)

    def c_rows(i, plane, e):
        lane = at.row_at(e) * 2 + at.core
        c_arrived(i, lane, plane)
        c_core(i, lane, plane)

    def c_arrived(i, lane, plane):
        cw.arrived(
            c_block(i, lane, plane),
            c_slot(i, lane, plane),
            at.device(at.plane, at.row, 1 - at.core),
        )

    def c_cores(i, row):
        for plane in range(planes):
            c_arrived(i, row * 2 + 1 - at.core, plane)

    def project(k):
        hidden = lax.dot_general(
            att_s[k], w_s[...], (((1,), (1,)), ((), ())), preferred_element_type=jnp.float32
        )
        rows = pl.ds(pl.multiple_of(at.lane * block, 16), block)
        cut = pl.ds(pl.multiple_of(at.plane * features, 128), features)
        hid_s[k, rows, cut] = hidden.astype(jnp.bfloat16)

    def normalize(k, quad):
        base = quad * QUAD * block

        @pl.loop(0, QUAD * block // WIDE)
        def _(j):
            rows = pl.ds(pl.multiple_of(base + j * WIDE, WIDE), WIDE)
            wide = hid_s[k, rows, :].astype(jnp.float32)
            square = jnp.sum(wide * wide, axis=1, keepdims=True)
            factor = lax.rsqrt(square / depth + EPSILON)
            out = pl.ds(pl.multiple_of(j * WIDE, WIDE), WIDE)
            factor_s[out] = jnp.broadcast_to(factor, (WIDE, 128))

        @pl.loop(0, QUAD * block // STEP)
        def _(j):
            rows = pl.ds(pl.multiple_of(base + j * STEP, STEP), STEP)
            out = pl.ds(pl.multiple_of(j * STEP, STEP), STEP)
            factor = factor_s[out]
            for c in range(depth // 128):
                cut = slice(c * 128, (c + 1) * 128)
                wide = hid_s[k, rows, cut].astype(jnp.float32)
                norm_s[out, cut] = (wide * factor * gain_ref[c : c + 1, :]).astype(jnp.bfloat16)

    first = [True]

    def score_group(k, quad, events, early=0):
        wait = first[0]
        first[0] = False
        tokens = QUAD * block
        start = (k * (at.lanes // QUAD) + quad) * tokens
        band = slice(start, start + tokens)

        def score(tile, size, split):
            if wait:
                load(tile, size).wait()
            part = size // split
            base = tile * TILE
            products = []
            for s in range(split):
                head = head_s[pl.ds(pl.multiple_of(base + s * part, 8), part)]
                products.append(
                    lax.dot_general(
                        head,
                        norm_s[...],
                        (((1,), (1,)), ((), ())),
                        preferred_element_type=jnp.float32,
                    )
                )
            for s, logits in enumerate(products):
                row_ = lax.broadcasted_iota(jnp.int32, logits.shape, 0)
                want = ids_s[:, band] - (base + s * part + at.me * vocab)
                chosen = jnp.where(row_ == want, logits, 0.0)
                cut = (part // 8, 8, tokens)
                before = max_s[:, band]
                best = jnp.maximum(before, jnp.max(logits.reshape(cut), axis=0))
                mass = jnp.sum(jnp.exp(logits.reshape(cut) - best[None]), axis=0)
                max_s[:, band] = best
                sum_s[:, band] = sum_s[:, band] * jnp.exp(before - best) + mass
                pick_s[:, band] += jnp.sum(chosen.reshape(cut), axis=0)

        @pl.loop(0, tiles + early)
        def _(step):
            for j, event in events:
                pl.when(step == j)(event)
            if early:
                pl.when(step >= early)(lambda: score(step - early, TILE, SPLIT))
            else:
                score(step, TILE, SPLIT)

        if rest:
            score(tiles, rest, 1)

    inner = jnp.logical_and(at.plane > 0, at.plane < planes - 1)
    outer = jnp.logical_not(inner)

    def b_relay(k):
        for source in sources:
            b_line.take(k, source)

    def b_wait(k):
        for source in sources:
            piece = b_piece(k, source)
            bw.arrived(piece, k * planes + source, at.device(source, at.row, at.core))

    def w_relay():
        for e in range(1, at.half):
            lane = at.row_at(e) * 2 + at.core
            for part in range(WPARTS):
                w_arrived(lane, part)
                w_core(lane, part)

    def w_wait():
        for row in range(at.half):
            lane = row * 2 + 1 - at.core
            for part in range(WPARTS):
                w_arrived(lane, part)

    def rows_take(k):
        for plane in [at.plane] + near:
            for e in range(1, at.half):
                c_rows(k, plane, e)

    def make_ids():
        for d in range(1, n):
            source = (at.me + d) % n
            meta.arrived(meta_all.at[source], source, source)
        for k in range(subs):
            i, h = k // halves, k % halves
            for quad in range(at.lanes // QUAD):
                got = [
                    meta_all[plane * at.lanes + lane][0:1, i * steps : (i + 1) * steps]
                    for lane in range(quad * QUAD, (quad + 1) * QUAD)
                    for plane in range(h * PAIR, (h + 1) * PAIR)
                ]
                start = (k * (at.lanes // QUAD) + quad) * QUAD * block
                ids_s[:, start : start + QUAD * block] = jnp.concatenate(got, axis=1).astype(
                    jnp.int32
                )

    def c_takes(k):
        for source in sources:
            c_take(k, source)

    def advance(k):
        project(k)
        c_own(k)

    def moment(inside, outside):
        return jnp.where(inner, inside, outside)

    assert planes == 4 and conts == 2
    peer = at.device(at.plane, at.row, 1 - at.core)

    attend(0)
    b_line.send_own(0)
    attend(1)
    b_line.send_own(1)
    attend(2)
    b_line.send_own(2)

    @pl.when(inner)
    def _():
        b_relay(0)

    attend(3)
    b_line.send_own(3)
    w_relay()

    @pl.when(inner)
    def _():
        b_relay(1)

    w_wait()

    @pl.when(outer)
    def _():
        b_wait(0)

    advance(0)

    def rate():
        shape = (n, 128)
        row_at = lax.broadcasted_iota(jnp.int32, shape, 0)
        lane_at = lax.broadcasted_iota(jnp.int32, shape, 1)
        groups = jnp.full(shape, -1, jnp.int32)
        for d in range(n):
            for i in range(conts):
                here = jnp.logical_and(row_at == d, lane_at == i)
                groups = jnp.where(here, group_ref[d * conts + i], groups)
        rewards = jnp.concatenate([meta_all[d][1:2, :] for d in range(n)], axis=0)

        def total(x):
            return jnp.sum(jnp.sum(x, axis=0, keepdims=True), axis=1, keepdims=True)

        for i in range(conts):
            same = (groups == group_ref[at.me * conts + i]).astype(jnp.float32)
            mean = total(same * rewards) / GROUP
            deviation = rewards - mean
            spread = jnp.sqrt(total(same * deviation * deviation) / (GROUP - 1))
            advantage = (reward_ref[i] - mean) / jnp.maximum(spread, REWARD_FLOOR)
            rating_s[i : i + 1, :] = jnp.broadcast_to(advantage, (1, 128))

    def settle():
        make_ids()
        kv.drain(kv_full(0, at.me), peer)
        meta.drain(meta_all.at[at.me], peer)
        qw.drain(q_piece(0, at.plane), peer)
        pw.drain(c_pieces(0, at.plane)[0], peer)
        ww.drain(w_full(at.lane, 0), peer)
        rate()

    def relays():
        b_relay(2)
        b_relay(3)

    def follow(k):
        pl.when(outer)(functools.partial(b_wait, k))
        advance(k)

    def ready(k):
        rows_take(k)
        for row in range(at.half):
            c_cores(k, row)
        normalize(k, 0)

    takes = [functools.partial(c_takes, k) for k in range(subs)]
    never = -1
    final = tiles + 2
    schedule = [
        [
            (moment(0, 1), settle),
            (moment(0, 1), takes[0]),
            (moment(1, never), relays),
            (moment(1, 0), functools.partial(follow, 1)),
            (moment(2, min(4, final)), functools.partial(follow, 2)),
            (moment(2, min(5, final)), takes[1]),
            (moment(3, min(5, final)), functools.partial(follow, 3)),
            (3, functools.partial(ready, 0)),
        ],
        [(min(1, tiles - 1), takes[2]), (min(2, tiles - 1), takes[3])],
        [(min(1, tiles - 1), functools.partial(rows_take, 3))],
        [],
    ]
    for k in range(subs):
        if k in (1, 2):
            rows_take(k)
        if k:
            for row in range(at.half):
                c_cores(k, row)
            normalize(k, 0)
        score_group(k, 0, schedule[k], 0 if k else 3)
        for quad in range(1, at.lanes // QUAD):
            normalize(k, quad)
            score_group(k, quad, [])

    tile_s[...] = jnp.zeros_like(tile_s)
    for i in range(conts):
        for lane in range(at.lanes):
            parts = [
                ((i * halves + h) * at.lanes + lane) * block for h in range(halves)
            ]

            def across(ref):
                return jnp.concatenate([ref[:, p : p + block] for p in parts], axis=1)

            peak = across(max_s)
            top = jnp.max(peak, axis=0, keepdims=True)
            mass = jnp.sum(across(sum_s) * jnp.exp(peak - top), axis=0, keepdims=True)
            tile_s[lane, i * 3 : i * 3 + 1] = top
            tile_s[lane, i * 3 + 1 : i * 3 + 2] = mass
            tile_s[lane, i * 3 + 2 : i * 3 + 3] = jnp.sum(across(pick_s), axis=0, keepdims=True)

    stat = Wire(stat_send, stat_recv)
    for d in range(1, n):
        target = (at.me + d) % n
        stat.send(tile_s.at[target % at.lanes], stats_s.at[at.me], at.me, target)
    own = pltpu.make_async_copy(tile_s.at[at.lane], stats_s.at[at.me], local_sem.at[0])
    own.start()
    bw.drain(b_piece(0, at.plane), peer)
    cw.drain(c_block(0, at.lane, at.plane), peer)
    for d in range(1, n):
        source = (at.me + d) % n
        stat.arrived(stats_s.at[source], source, source)
    own.wait()
    advantages = jnp.zeros((1, 128), jnp.float32)
    objectives = jnp.zeros((1, 128), jnp.float32)
    for i in range(conts):
        peaks = stats_s[:, i * 3, :]
        top = jnp.max(peaks, axis=0, keepdims=True)
        mass = jnp.sum(stats_s[:, i * 3 + 1, :] * jnp.exp(peaks - top), axis=0, keepdims=True)
        picked = jnp.sum(stats_s[:, i * 3 + 2, :], axis=0, keepdims=True)
        every = picked - top - jnp.log(mass)
        logprob = pick([every[:, p * steps : (p + 1) * steps] for p in range(planes)], at.plane)
        length = length_own_ref[i]
        position = lax.broadcasted_iota(jnp.int32, logprob.shape, 1)
        logprob = jnp.where(position < length, logprob, 0.0)
        logprob_out[i : i + 1, :] = logprob
        advantage = rating_s[i : i + 1, :]
        summed = jnp.sum(logprob, axis=1, keepdims=True)
        objective = advantage * summed / jnp.full((1, 128), length, jnp.int32).astype(jnp.float32)
        advantages = jnp.where(lane_of == i, advantage, advantages)
        objectives = jnp.where(lane_of == i, objective, objectives)
    rating_out[0:1, :] = advantages[:, :conts]
    rating_out[1:2, :] = objectives[:, :conts]
    stat.drain(stats_s.at[at.me], peer)


def layer(n, planes, groups, lengths, own, rewards, q, ck, cv, pk, pv, ids, w, gain, head):
    conts, steps, width = q.shape
    prompts, span, _ = pk.shape
    lanes = n // planes
    half = lanes // 2
    depth = w.shape[1]
    block = planes * steps
    total = conts * lanes * block
    sub = PAIR * steps
    subs = conts * planes // PAIR
    dma = pltpu.SemaphoreType.DMA
    vmem = pl.BlockSpec(memory_space=VMEM)
    smem = pl.BlockSpec(memory_space=pltpu.SMEM)
    bf16, f32 = jnp.bfloat16, jnp.float32
    running = VMEM((8, total), f32)
    shape = jax.ShapeDtypeStruct
    kv_sends = 2 * prompts * ((planes - 1) + half + (planes - 1) * half + planes * (half - 1))
    line_sends = 3 + planes - 1
    return pl.pallas_call(
        functools.partial(layer_kernel, n, planes),
        out_shape=(shape((conts, steps), f32), shape((2, conts), f32)),
        in_specs=[smem] * 4 + [vmem] * 8 + [pl.BlockSpec(memory_space=pl.ANY)],
        out_specs=(vmem, vmem),
        scratch_shapes=[
            VMEM((n, 8, 128), f32),
            VMEM((8, 128), f32),
            VMEM((n, 8, 128), f32),
            VMEM((conts, 128), f32),
            VMEM((conts, planes, steps, width // planes), bf16),
            VMEM((conts, planes, steps, HD), bf16),
            VMEM((conts, planes, steps, HD), bf16),
            VMEM((prompts, span * n, HD), bf16),
            VMEM((prompts, span * n, HD), bf16),
            VMEM((subs, sub, width), bf16),
            VMEM((w.shape[0] * lanes, depth), bf16),
            VMEM((subs, lanes * sub, depth), bf16),
            VMEM((QUAD * sub, depth), bf16),
            VMEM((QUAD * sub, 128), f32),
            VMEM(head.shape, bf16),
            VMEM((1, total), jnp.int32),
            running,
            running,
            running,
            VMEM((lanes, 8, 128), f32),
            dma((kv_sends,)),
            dma((2 * prompts * n,)),
            dma((conts * (planes - 1),)),
            dma((conts * planes,)),
            dma((2 * conts * (planes - 1),)),
            dma((2 * conts * planes,)),
            dma((n - 1,)),
            dma((n,)),
            dma((2 * half * WPARTS,)),
            dma((lanes * WPARTS,)),
            dma((subs * line_sends,)),
            dma((subs * planes,)),
            dma((subs * (line_sends + planes * half + planes * (half - 1)),)),
            dma((subs * n,)),
            dma((n - 1,)),
            dma((n,)),
            dma((2 * prompts + 1 + 3 * conts + 1,)),
            dma((pl.cdiv(head.shape[0], TILE),)),
        ],
        compiler_params=pltpu.CompilerParams(
            collective_id=0, has_side_effects=True, vmem_limit_bytes=LIMIT
        ),
        name="layer",
    )(groups, lengths, own, rewards, q, ck, cv, pk, pv, ids, w, gain, head)


def per_device(
    n,
    cont_query,
    cont_key,
    cont_value,
    prefix_key,
    prefix_value,
    out_weight,
    norm_gain,
    lm_head,
    target_ids,
    cont_len,
    prompt_len,
    group_of,
    rewards,
):
    token_logprob, rating = layer(
        n,
        cont_key.shape[2] // HD,
        group_of,
        prompt_len,
        cont_len,
        rewards,
        cont_query,
        cont_key,
        cont_value,
        prefix_key,
        prefix_value,
        target_ids,
        out_weight.T,
        norm_gain.reshape(-1, 128),
        lm_head.T,
    )
    return (token_logprob, rating[0], rating[1])


def solution(mesh):
    placed = (
        P(("grp", "seq"), None, None),
        P(("grp", "seq"), None, None),
        P(("grp", "seq"), None, None),
        P("grp", "seq", None),
        P("grp", "seq", None),
        P(None, "seq"),
        P(),
        P(None, "seq"),
        P(("grp", "seq"), None),
        P(("grp", "seq")),
        P("grp"),
        P("grp"),
        P(("grp", "seq")),
    )
    return jax.shard_map(
        functools.partial(per_device, mesh.shape["seq"]),
        mesh=mesh,
        in_specs=placed,
        out_specs=(P(("grp", "seq"), None), P(("grp", "seq")), P(("grp", "seq"))),
        check_vma=False,
    )
```

profile of v0, /device:TPU:0, one launch (start us, length us, event | category | flops | bytes accessed | tf_op | source)
XLA Modules:
  0.0 121.2 jit_solution(9325726231324714743)
XLA Ops:
  0.6 118.0 %layer.1 = (f32[2,32]{1,0:T(2,128)}, f32[2,2]{1,0:T(2,128)}) custom-call(s32[32]{0:T(128)} %group_ref.1, s32[2]{0:T(128)} %length_ref.1, s32[2]{0:T(128)} %length_own_ref.1, f32[2]{0:T(128)} %reward_ref.1, bf16[2,32,2560]{2,1,0:T(8,128)(2,1)} %q_ref.1, bf16[2,32,512]{2,1,0:T(8,128)(2,1)} %ck_ref.1, bf16[2,32,512]{2,1,0:T(8,128)(2,1)} %cv_ref.1, ...), custom_call_target="tpu_custom_call" | custom-call | tf_op jit(solution)/shard_map/layer/pallas_call | solution.py:824
  118.7 1.3 %slice_bitcast_fusion = (f32[2]{0:T(128)}, f32[2]{0:T(128)}) fusion(f32[2,2]{1,0:T(2,128)} %get-tuple-element.6), kind=kLoop, calls=%fused_computation | loop fusion | bytes 32 | tf_op jit(solution)/shard_map/squeeze | solution.py:909
  119.9 1.2 %copy.17 = f32[2,32]{1,0:T(2,128)} copy(f32[2,32]{1,0:T(2,128)} %get-tuple-element.12) | data formatting | bytes 512
where the time goes:
time: 121 us
  Pallas kernels  118 us (98%)
  local copies, waits for them, and re-layouts  2.48 us (2%)
    pallas_call x1, Pallas kernels, layer(): pl.pallas_call(functools.partial(layer_kernel, n, planes), out_shape=(sha...  118 us

commit v1 on v0

--- a/solution.py
+++ b/solution.py
@@ -75,45 +75,46 @@
 
 
 class Wire:
-    def __init__(self, send_sem, recv_sem):
-        self.send_sem, self.recv_sem = send_sem, recv_sem
+    def __init__(self, send_sem, recv_sem, shared=0):
+        self.send_sem, self.recv_sem, self.shared = send_sem, recv_sem, shared
         self.sent = []
 
-    def send(self, src, dst, slot, target, when=None):
+    def send(self, src, dst, slot, target, when=None, share=None):
+        if share is None:
+            share = self.shared + len(self.sent)
+            self.sent.append(when)
         copy = pltpu.make_async_remote_copy(
             src_ref=src,
             dst_ref=dst,
-            send_sem=self.send_sem.at[len(self.sent)],
+            send_sem=self.send_sem.at[share],
             recv_sem=self.recv_sem.at[slot],
             device_id={"seq": target},
             device_id_type=MESH,
         )
-        self.sent.append(when)
         if when is None:
             copy.start()
         else:
             pl.when(when())(copy.start)
 
-    def arrived(self, dst, slot, other):
-        pltpu.make_async_remote_copy(
-            src_ref=dst,
-            dst_ref=dst,
-            send_sem=self.send_sem.at[0],
+    def whole(self, ref, send, slot, other):
+        return pltpu.make_async_remote_copy(
+            src_ref=ref,
+            dst_ref=ref,
+            send_sem=self.send_sem.at[send],
             recv_sem=self.recv_sem.at[slot],
             device_id={"seq": other},
             device_id_type=MESH,
-        ).wait_recv()
+        )
+
+    def arrived(self, dst, slot, other):
+        self.whole(dst, 0, slot, other).wait_recv()
+
+    def left(self, ref, send, other):
+        self.whole(ref, send, 0, other).wait_send()
 
     def drain(self, like, other):
         for i, when in enumerate(self.sent):
-            copy = pltpu.make_async_remote_copy(
-                src_ref=like,
-                dst_ref=like,
-                send_sem=self.send_sem.at[i],
-                recv_sem=self.recv_sem.at[0],
-                device_id={"seq": other},
-                device_id_type=MESH,
-            )
+            copy = self.whole(like, self.shared + i, 0, other)
             if when is None:
                 copy.wait_send()
             else:
@@ -127,24 +128,24 @@
     def peer(self, plane):
         return self.at.device(plane, self.at.row, self.at.core)
 
-    def send_own(self, part):
+    def send_own(self, part, far=True):
         at = self.at
         last = at.planes - 1
         mine = self.piece(part, at.plane)
         slot = self.slot(part, at.plane)
         moves = [(1, lambda: at.plane < last), (-1, lambda: at.plane > 0)]
-        if at.planes > 2:
-            far = jnp.where(at.plane == 0, 2, last - 2)
+        if at.planes > 2 and far:
+            beyond = jnp.where(at.plane == 0, 2, last - 2)
 
             def ends():
                 return jnp.logical_or(at.plane == 0, at.plane == last)
 
-            self.wire.send(mine, mine, slot, self.peer(far), ends)
+            self.wire.send(mine, mine, slot, self.peer(beyond), ends)
         for step, when in moves:
             target = jnp.clip(at.plane + step, 0, last)
             self.wire.send(mine, mine, slot, self.peer(target), when)
 
-    def take(self, part, source):
+    def take(self, part, source, chain=False):
         at = self.at
         last = at.planes - 1
         got = self.piece(part, source)
@@ -156,6 +157,8 @@
         def when():
             target = toward()
             inside = jnp.logical_and(target >= 0, target <= last)
+            if chain:
+                return inside
             direct = jnp.logical_or(
                 jnp.logical_and(source == 0, at.plane == 1),
                 jnp.logical_and(source == last, at.plane == last - 1),
@@ -181,8 +184,7 @@
     w_ref,
     gain_ref,
     head_hbm,
-    logprob_out,
-    rating_out,
+    result_out,
     stats_s,
     meta_s,
     meta_all,
@@ -278,59 +280,73 @@
 
     def kv_full(part, source):
         start = pl.multiple_of(source * span, 16)
-        return (pk_s, pv_s)[part // prompts].at[part % prompts, pl.ds(start, span), :]
+        return (pk_s, pv_s)[part].at[:, pl.ds(start, span), :]
 
     def kv_own(part, plane):
         cut = pl.ds(pl.multiple_of(plane * HD, 128), HD)
-        return (pk_ref, pv_ref)[part // prompts].at[part % prompts, :, cut]
-
-    def kv_share(part, source, src, core_only=False):
-        slot = part * n + source
+        return (pk_ref, pv_ref)[part].at[:, :, cut]
+
+    kinds = planes + (at.half - 1) * planes + 1
+
+    def z_slot(part, plane):
+        return part * kinds + plane
+
+    def row_slot(part, e, plane):
+        return part * kinds + planes + (e - 1) * planes + plane
+
+    def core_slot(part):
+        return part * kinds + kinds - 1
+
+    def kv_core(part, source, src):
         dst = kv_full(part, source)
-        if not core_only:
-            for e in range(1, at.half):
-                kv.send(src, dst, slot, at.device(at.plane, at.row_at(e), at.core))
-        kv.send(src, dst, slot, at.device(at.plane, at.row, 1 - at.core))
-
-    ww = Wire(w_send, w_recv)
+        target = at.device(at.plane, at.row, 1 - at.core)
+        kv.send(src, dst, core_slot(part), target, share=part)
+
+    def kv_share(part, source, plane, src):
+        for e in range(1, at.half):
+            target = at.device(at.plane, at.row_at(e), at.core)
+            slot = row_slot(part, at.half - e, plane)
+            kv.send(src, kv_full(part, source), slot, target, share=part)
+        kv_core(part, source, src)
+
+    ww = Wire(w_send, w_recv, at.half - 1)
     wpart = wrows // WPARTS
 
-    def w_full(lane, k):
-        start = pl.multiple_of(lane * wrows + k * wpart, 16)
-        return w_s.at[pl.ds(start, wpart)]
-
-    def w_core(lane, k):
-        piece = w_full(lane, k)
-        ww.send(piece, piece, lane * WPARTS + k, at.device(at.plane, at.row, 1 - at.core))
+    def w_full(lane):
+        return w_s.at[pl.ds(pl.multiple_of(lane * wrows, 16), wrows)]
 
     def w_own(k):
-        src = w_ref.at[pl.ds(k * wpart, wpart)]
-        slot = at.lane * WPARTS + k
+        start = pl.multiple_of(at.lane * wrows + k * wpart, 16)
+        src, dst = w_ref.at[pl.ds(k * wpart, wpart)], w_s.at[pl.ds(start, wpart)]
         for e in range(1, at.half):
-            ww.send(src, w_full(at.lane, k), slot, at.device(at.plane, at.row_at(e), at.core))
-        ww.send(src, w_full(at.lane, k), slot, at.device(at.plane, at.row, 1 - at.core))
-
-    def w_arrived(lane, k):
+            target = at.device(at.plane, at.row_at(e), at.core)
+            ww.send(src, dst, at.lane, target, share=e - 1)
+
+    def w_core(lane, src):
         other = at.device(at.plane, at.row, 1 - at.core)
-        ww.arrived(w_full(lane, k), lane * WPARTS + k, other)
-
-    for part in range(2 * prompts):
+        ww.send(src, w_full(lane), lane, other)
+
+    def w_arrived(lane):
+        ww.arrived(w_full(lane), lane, at.device(at.plane, at.row, 1 - at.core))
+
+    for part in range(2):
         for target in far:
             kv.send(
                 kv_own(part, target),
                 kv_full(part, at.me),
-                part * n + at.me,
+                z_slot(part, at.plane),
                 at.device(target, at.row, at.core),
+                share=part,
             )
         own = kv_own(part, at.plane)
-        kv_share(part, at.me, own)
+        kv_share(part, at.me, at.plane, own)
         local(own, kv_full(part, at.me))
-    w_own(0)
-    w_own(1)
+    for k in range(2):
+        w_own(k)
 
     meta = Wire(meta_send, meta_recv)
     for d in range(1, n):
-        meta.send(meta_s, meta_all.at[at.me], at.me, (at.me + d) % n)
+        meta.send(meta_s, meta_all.at[at.me], 0, (at.me + d) % n, share=0)
     local(meta_s, meta_all.at[at.me])
 
     qw = Wire(q_send, q_recv)
@@ -369,32 +385,35 @@
     def kv_from_rows(plane, part):
         for e in range(1, at.half):
             source = at.device(plane, at.row_at(e), at.core)
-            kv.arrived(kv_full(part, source), part * n + source, source)
-            kv_share(part, source, kv_full(part, source), core_only=True)
+            kv.arrived(kv_full(part, source), row_slot(part, e, plane), source)
+            kv_core(part, source, kv_full(part, source))
 
     def kv_from_plane(plane, part):
         source = at.device(plane, at.row, at.core)
-        kv.arrived(kv_full(part, source), part * n + source, source)
-        kv_share(part, source, kv_full(part, source))
-
-    for part in range(2 * prompts):
+        kv.arrived(kv_full(part, source), z_slot(part, plane), source)
+        kv_share(part, source, plane, kv_full(part, source))
+
+    for part in range(2):
         for plane in near:
             kv_from_plane(plane, part)
-        if part == prompts - 1:
-            w_own(2)
         if part:
             for plane in [at.plane] + near:
                 kv_from_rows(plane, part - 1)
+        else:
+            w_own(2)
     for k in range(3, WPARTS):
         w_own(k)
+    w_core(at.lane, w_ref)
     for plane in [at.plane] + near:
-        kv_from_rows(plane, 2 * prompts - 1)
-
-    for part in range(2 * prompts):
-        for plane in range(planes):
-            for row in range(at.half):
-                source = at.device(plane, row, 1 - at.core)
-                kv.arrived(kv_full(part, source), part * n + source, source)
+        kv_from_rows(plane, 1)
+
+    peer = at.device(at.plane, at.row, 1 - at.core)
+
+    def kv_many(part, count):
+        return (pk_s, pv_s)[part].at[:, pl.ds(0, count * span), :]
+
+    for part in range(2):
+        kv.arrived(kv_many(part, n // 2), core_slot(part), peer)
     for copy in locals_:
         copy.wait()
 
@@ -453,36 +472,29 @@
 
     b_line = Line(at, bw, b_piece, lambda i, plane: i * planes + plane)
 
-    cw = Wire(c_send, c_recv)
+    cw = Wire(c_send, c_recv, subs)
 
     def c_block(i, lane, plane):
         rows = pl.ds(pl.multiple_of(lane * block, 16), block)
         cut = pl.ds(pl.multiple_of(plane * features, 128), features)
         return hid_s.at[i, rows, cut]
 
-    def c_slot(i, lane, plane):
-        return i * n + plane * at.lanes + lane
-
     c_line = Line(
         at,
         cw,
         lambda i, plane: c_block(i, at.lane, plane),
-        lambda i, plane: c_slot(i, at.lane, plane),
+        z_slot,
     )
 
     def c_core(i, lane, plane):
         piece = c_block(i, lane, plane)
-        cw.send(piece, piece, c_slot(i, lane, plane), at.device(at.plane, at.row, 1 - at.core))
+        cw.send(piece, piece, core_slot(i), peer, share=i)
 
     def c_share(i, plane):
         piece = c_block(i, at.lane, plane)
         for e in range(1, at.half):
-            cw.send(
-                piece,
-                piece,
-                c_slot(i, at.lane, plane),
-                at.device(at.plane, at.row_at(e), at.core),
-            )
+            target = at.device(at.plane, at.row_at(e), at.core)
+            cw.send(piece, piece, row_slot(i, at.half - e, plane), target, share=i)
         c_core(i, at.lane, plane)
 
     def c_own(i):
@@ -493,21 +505,20 @@
         c_line.take(i, plane)
         c_share(i, plane)
 
+    def c_receive(i, plane):
+        cw.arrived(c_block(i, at.lane, plane), z_slot(i, plane), peer)
+        c_share(i, plane)
+
     def c_rows(i, plane, e):
         lane = at.row_at(e) * 2 + at.core
-        c_arrived(i, lane, plane)
+        cw.arrived(c_block(i, lane, plane), row_slot(i, e, plane), peer)
         c_core(i, lane, plane)
 
-    def c_arrived(i, lane, plane):
-        cw.arrived(
-            c_block(i, lane, plane),
-            c_slot(i, lane, plane),
-            at.device(at.plane, at.row, 1 - at.core),
-        )
-
-    def c_cores(i, row):
-        for plane in range(planes):
-            c_arrived(i, row * 2 + 1 - at.core, plane)
+    def c_many(i, count):
+        return hid_s.at[i, pl.ds(0, count * block), :]
+
+    def c_cores(i):
+        cw.arrived(c_many(i, at.half), core_slot(i), peer)
 
     def project(k):
         hidden = lax.dot_general(
@@ -592,26 +603,34 @@
     outer = jnp.logical_not(inner)
 
     def b_relay(k):
-        for source in sources:
+        for source in sources[:-1]:
             b_line.take(k, source)
 
+    def b_arrived(k, source):
+        piece = b_piece(k, source)
+        bw.arrived(piece, k * planes + source, at.device(source, at.row, at.core))
+
     def b_wait(k):
-        for source in sources:
-            piece = b_piece(k, source)
-            bw.arrived(piece, k * planes + source, at.device(source, at.row, at.core))
+        @pl.when(outer)
+        def _():
+            for source in sources:
+                b_arrived(k, source)
+
+        if k < 2:
+
+            @pl.when(inner)
+            def _():
+                b_arrived(k, sources[-1])
 
     def w_relay():
         for e in range(1, at.half):
             lane = at.row_at(e) * 2 + at.core
-            for part in range(WPARTS):
-                w_arrived(lane, part)
-                w_core(lane, part)
+            w_arrived(lane)
+            w_core(lane, w_full(lane))
 
     def w_wait():
         for row in range(at.half):
-            lane = row * 2 + 1 - at.core
-            for part in range(WPARTS):
-                w_arrived(lane, part)
+            w_arrived(row * 2 + 1 - at.core)
 
     def rows_take(k):
         for plane in [at.plane] + near:
@@ -619,9 +638,7 @@
                 c_rows(k, plane, e)
 
     def make_ids():
-        for d in range(1, n):
-            source = (at.me + d) % n
-            meta.arrived(meta_all.at[source], source, source)
+        meta.arrived(meta_all.at[pl.ds(0, n - 1)], 0, peer)
         for k in range(subs):
             i, h = k // halves, k % halves
             for quad in range(at.lanes // QUAD):
@@ -647,21 +664,19 @@
         return jnp.where(inner, inside, outside)
 
     assert planes == 4 and conts == 2
-    peer = at.device(at.plane, at.row, 1 - at.core)
-
     attend(0)
     b_line.send_own(0)
     attend(1)
     b_line.send_own(1)
     attend(2)
-    b_line.send_own(2)
+    b_line.send_own(2, far=False)
 
     @pl.when(inner)
     def _():
         b_relay(0)
 
     attend(3)
-    b_line.send_own(3)
+    b_line.send_own(3, far=False)
     w_relay()
 
     @pl.when(inner)
@@ -669,12 +684,13 @@
         b_relay(1)
 
     w_wait()
-
-    @pl.when(outer)
+    b_wait(0)
+    advance(0)
+
+    @pl.when(inner)
     def _():
-        b_wait(0)
-
-    advance(0)
+        for k in (2, 3):
+            b_line.take(k, sources[-1], chain=True)
 
     def rate():
         shape = (n, 128)
@@ -700,51 +716,72 @@
 
     def settle():
         make_ids()
-        kv.drain(kv_full(0, at.me), peer)
-        meta.drain(meta_all.at[at.me], peer)
+        for part in range(2):
+            kv.left(kv_many(part, n - 1), part, peer)
+        meta.left(meta_all.at[pl.ds(0, n - 1)], 0, peer)
         qw.drain(q_piece(0, at.plane), peer)
         pw.drain(c_pieces(0, at.plane)[0], peer)
-        ww.drain(w_full(at.lane, 0), peer)
+        for e in range(1, at.half):
+            ww.left(w_full(at.lane), e - 1, peer)
+        ww.drain(w_full(at.lane), peer)
         rate()
 
-    def relays():
-        b_relay(2)
-        b_relay(3)
-
     def follow(k):
-        pl.when(outer)(functools.partial(b_wait, k))
+        b_wait(k)
         advance(k)
 
     def ready(k):
         rows_take(k)
-        for row in range(at.half):
-            c_cores(k, row)
+        c_cores(k)
         normalize(k, 0)
 
-    takes = [functools.partial(c_takes, k) for k in range(subs)]
-    never = -1
-    final = tiles + 2
+    def taking(k, *which):
+        def take():
+            for j in which:
+                c_take(k, sources[j])
+
+        return take
+
+    def receiving(k):
+        for plane in sources:
+            c_receive(k, plane)
+
+    def sent():
+        bw.drain(b_piece(0, at.plane), peer)
+        cw.drain(c_block(0, at.lane, at.plane), peer)
+        for k in range(subs):
+            cw.left(c_many(k, at.lanes - 1), k, peer)
+
+    def at_step(j, early=0):
+        return min(j, tiles - 1) + early
+
     schedule = [
         [
             (moment(0, 1), settle),
-            (moment(0, 1), takes[0]),
-            (moment(1, never), relays),
+            (moment(0, 1), taking(0, 0, 1, 2)),
             (moment(1, 0), functools.partial(follow, 1)),
-            (moment(2, min(4, final)), functools.partial(follow, 2)),
-            (moment(2, min(5, final)), takes[1]),
-            (moment(3, min(5, final)), functools.partial(follow, 3)),
+            (moment(1, -1), functools.partial(b_relay, 2)),
+            (moment(2, -1), taking(1, 0, 1, 2)),
+            (moment(-1, at_step(1, 3)), functools.partial(receiving, 1)),
+            (moment(2, at_step(1, 3)), functools.partial(follow, 2)),
+            (moment(3, -1), functools.partial(b_relay, 3)),
+            (moment(3, at_step(2, 3)), functools.partial(follow, 3)),
             (3, functools.partial(ready, 0)),
+            (moment(at_step(2, 3), -1), taking(2, 0, 1, 2)),
         ],
-        [(min(1, tiles - 1), takes[2]), (min(2, tiles - 1), takes[3])],
-        [(min(1, tiles - 1), functools.partial(rows_take, 3))],
-        [],
+        [
+            (moment(-1, 0), functools.partial(receiving, 2)),
+            (moment(0, at_step(2)), taking(3, 0, 1, 2)),
+            (at_step(2), functools.partial(rows_take, 2)),
+        ],
+        [(at_step(2), functools.partial(rows_take, 3))],
+        [(at_step(1), sent)],
     ]
     for k in range(subs):
-        if k in (1, 2):
+        if k == 1:
             rows_take(k)
         if k:
-            for row in range(at.half):
-                c_cores(k, row)
+            c_cores(k)
             normalize(k, 0)
         score_group(k, 0, schedule[k], 0 if k else 3)
         for quad in range(1, at.lanes // QUAD):
@@ -771,14 +808,10 @@
     stat = Wire(stat_send, stat_recv)
     for d in range(1, n):
         target = (at.me + d) % n
-        stat.send(tile_s.at[target % at.lanes], stats_s.at[at.me], at.me, target)
+        stat.send(tile_s.at[target % at.lanes], stats_s.at[at.me], 0, target, share=0)
     own = pltpu.make_async_copy(tile_s.at[at.lane], stats_s.at[at.me], local_sem.at[0])
     own.start()
-    bw.drain(b_piece(0, at.plane), peer)
-    cw.drain(c_block(0, at.lane, at.plane), peer)
-    for d in range(1, n):
-        source = (at.me + d) % n
-        stat.arrived(stats_s.at[source], source, source)
+    stat.arrived(stats_s.at[pl.ds(0, n - 1)], 0, peer)
     own.wait()
     advantages = jnp.zeros((1, 128), jnp.float32)
     objectives = jnp.zeros((1, 128), jnp.float32)
@@ -792,15 +825,15 @@
         length = length_own_ref[i]
         position = lax.broadcasted_iota(jnp.int32, logprob.shape, 1)
         logprob = jnp.where(position < length, logprob, 0.0)
-        logprob_out[i : i + 1, :] = logprob
+        result_out[i : i + 1, :steps] = logprob
         advantage = rating_s[i : i + 1, :]
         summed = jnp.sum(logprob, axis=1, keepdims=True)
         objective = advantage * summed / jnp.full((1, 128), length, jnp.int32).astype(jnp.float32)
         advantages = jnp.where(lane_of == i, advantage, advantages)
         objectives = jnp.where(lane_of == i, objective, objectives)
-    rating_out[0:1, :] = advantages[:, :conts]
-    rating_out[1:2, :] = objectives[:, :conts]
-    stat.drain(stats_s.at[at.me], peer)
+    result_out[conts : conts + 1, :] = advantages
+    result_out[conts + 1 : conts + 2, :] = objectives
+    stat.left(stats_s.at[pl.ds(0, n - 1)], 0, peer)
 
 
 def layer(n, planes, groups, lengths, own, rewards, q, ck, cv, pk, pv, ids, w, gain, head):
@@ -819,13 +852,13 @@
     bf16, f32 = jnp.bfloat16, jnp.float32
     running = VMEM((8, total), f32)
     shape = jax.ShapeDtypeStruct
-    kv_sends = 2 * prompts * ((planes - 1) + half + (planes - 1) * half + planes * (half - 1))
+    kinds = planes + (half - 1) * planes + 1
     line_sends = 3 + planes - 1
     return pl.pallas_call(
         functools.partial(layer_kernel, n, planes),
-        out_shape=(shape((conts, steps), f32), shape((2, conts), f32)),
+        out_shape=shape((conts + 2, 128), f32),
         in_specs=[smem] * 4 + [vmem] * 8 + [pl.BlockSpec(memory_space=pl.ANY)],
-        out_specs=(vmem, vmem),
+        out_specs=vmem,
         scratch_shapes=[
             VMEM((n, 8, 128), f32),
             VMEM((8, 128), f32),
@@ -847,23 +880,23 @@
             running,
             running,
             VMEM((lanes, 8, 128), f32),
-            dma((kv_sends,)),
-            dma((2 * prompts * n,)),
+            dma((2,)),
+            dma((2 * kinds,)),
             dma((conts * (planes - 1),)),
             dma((conts * planes,)),
             dma((2 * conts * (planes - 1),)),
             dma((2 * conts * planes,)),
-            dma((n - 1,)),
-            dma((n,)),
-            dma((2 * half * WPARTS,)),
-            dma((lanes * WPARTS,)),
+            dma((1,)),
+            dma((1,)),
+            dma((2 * half - 1,)),
+            dma((lanes,)),
             dma((subs * line_sends,)),
             dma((subs * planes,)),
-            dma((subs * (line_sends + planes * half + planes * (half - 1)),)),
-            dma((subs * n,)),
-            dma((n - 1,)),
-            dma((n,)),
-            dma((2 * prompts + 1 + 3 * conts + 1,)),
+            dma((subs * (1 + line_sends),)),
+            dma((subs * kinds,)),
+            dma((1,)),
+            dma((1,)),
+            dma((2 + 1 + 3 * conts + 1,)),
             dma((pl.cdiv(head.shape[0], TILE),)),
         ],
         compiler_params=pltpu.CompilerParams(
@@ -889,7 +922,8 @@
     group_of,
     rewards,
 ):
-    token_logprob, rating = layer(
+    conts, steps, _ = cont_query.shape
+    result = layer(
         n,
         cont_key.shape[2] // HD,
         group_of,
@@ -906,7 +940,7 @@
         norm_gain.reshape(-1, 128),
         lm_head.T,
     )
-    return (token_logprob, rating[0], rating[1])
+    return (result[:conts, :steps], result[conts, :conts], result[conts + 1, :conts])
 
 
 def solution(mesh):

time: 121 us -> 114 us (0.942)
  Pallas kernels: 118 us -> 111 us
    pallas_call x1, Pallas kernels: 118 us -> 111 us  [layer(): pl.pallas_call(functools.partial(layer_kernel, n, planes), out_shape=shap...]
    slice x0 -> x1, local copies, waits for them, and re-layouts: none -> 1.23 us  [per_device(): result[:conts, :steps]]
    unnamed x1 -> x0, local copies, waits for them, and re-layouts: 1.22 us -> none
where the time goes in v1:
time: 114 us
  Pallas kernels  111 us (97%)
  local copies, waits for them, and re-layouts  2.5 us (2%)
    pallas_call x1, Pallas kernels, layer(): pl.pallas_call(functools.partial(layer_kernel, n, planes), out_shape=shap...  111 us

profile of v1, /device:TPU:0, one launch (start us, length us, event | category | flops | bytes accessed | tf_op | source)
XLA Modules:
  0.0 114.2 jit_solution(13781800486249312872)
XLA Ops:
  0.6 111.0 %layer.1 = f32[4,128]{1,0:T(4,128)} custom-call(s32[32]{0:T(128)} %group_ref.1, s32[2]{0:T(128)} %length_ref.1, s32[2]{0:T(128)} %length_own_ref.1, f32[2]{0:T(128)} %reward_ref.1, bf16[2,32,2560]{2,1,0:T(8,128)(2,1)} %q_ref.1, bf16[2,32,512]{2,1,0:T(8,128)(2,1)} %ck_ref.1, bf16[2,32,512]{2,1,0:T(8,128)(2,1)} %cv_ref.1, bf16[2,128,512]{2,1,0:T(8,128)(2,1)} %pk_ref.1, ...), custom_call_target="tpu_custom_call" | custom-call | tf_op jit(solution)/shard_map/layer/pallas_call | solution.py:857
  111.7 1.3 %slice_bitcast_fusion = (f32[2]{0:T(128)}, f32[2]{0:T(128)}) fusion(f32[4,128]{1,0:T(4,128)} %layer.1), kind=kLoop, calls=%fused_computation | loop fusion | bytes 32 | tf_op jit(solution)/shard_map/squeeze | solution.py:943
  113.0 1.2 %slice.9 = f32[2,32]{1,0:T(2,128)} slice(f32[4,128]{1,0:T(4,128)} %layer.1), slice={[0:2], [0:32]} | slice | bytes 512 | tf_op jit(solution)/shard_map/slice | solution.py:943

commit v2 on v1

--- a/solution.py
+++ b/solution.py
@@ -906,6 +906,29 @@
     )(groups, lengths, own, rewards, q, ck, cv, pk, pv, ids, w, gain, head)
 
 
+def finish_kernel(result_ref, logprob_ref, advantage_ref, objective_ref):
+    conts, steps = logprob_ref.shape
+    logprob_ref[...] = result_ref[:conts, :steps]
+    advantage_ref[...] = result_ref[conts : conts + 1, :conts]
+    objective_ref[...] = result_ref[conts + 1 : conts + 2, :conts]
+
+
+def finish(conts, steps, result):
+    vmem = pl.BlockSpec(memory_space=VMEM)
+    shape = jax.ShapeDtypeStruct
+    return pl.pallas_call(
+        finish_kernel,
+        out_shape=(
+            shape((conts, steps), jnp.float32),
+            shape((1, conts), jnp.float32),
+            shape((1, conts), jnp.float32),
+        ),
+        in_specs=[vmem],
+        out_specs=(vmem, vmem, vmem),
+        name="finish",
+    )(result)
+
+
 def per_device(
     n,
     cont_query,
@@ -940,7 +963,8 @@
         norm_gain.reshape(-1, 128),
         lm_head.T,
     )
-    return (result[:conts, :steps], result[conts, :conts], result[conts + 1, :conts])
+    logprob, advantage, objective = finish(conts, steps, result)
+    return (logprob, advantage.reshape(conts), objective.reshape(conts))
 
 
 def solution(mesh):

time: 114 us -> 113 us (level)
  local copies, waits for them, and re-layouts: 2.5 us -> 0 us
    squeeze x1 -> x0, local copies, waits for them, and re-layouts: 1.27 us -> none  [per_device(): result[conts + 1, :conts]]
    pallas_call x0 -> x1, Pallas kernels: none -> 1.24 us  [finish(): pl.pallas_call(finish_kernel, out_shape=(shape((conts, steps), jnp.float3...]
    slice x1 -> x0, local copies, waits for them, and re-layouts: 1.23 us -> none  [per_device(): result[:conts, :steps]]
where the time goes in v2:
time: 113 us
  Pallas kernels  112 us (99%)
    pallas_call x1, Pallas kernels, layer(): pl.pallas_call(functools.partial(layer_kernel, n, planes), out_shape=shap...  111 us

profile of v2, /device:TPU:0, one launch (start us, length us, event | category | flops | bytes accessed | tf_op | source)
XLA Modules:
  0.0 112.9 jit_solution(4520277686740732741)
XLA Ops:
  0.6 111.0 %layer.1.result_ref = f32[4,128]{1,0:T(4,128)} custom-call(s32[32]{0:T(128)} %group_ref.1, s32[2]{0:T(128)} %length_ref.1, s32[2]{0:T(128)} %length_own_ref.1, f32[2]{0:T(128)} %reward_ref.1, bf16[2,32,2560]{2,1,0:T(8,128)(2,1)} %q_ref.1, bf16[2,32,512]{2,1,0:T(8,128)(2,1)} %ck_ref.1, bf16[2,32,512]{2,1,0:T(8,128)(2,1)} %cv_ref.1, ...), custom_call_target="tpu_custom_call" | custom-call | tf_op jit(solution)/shard_map/layer/pallas_call | solution.py:857
  111.7 1.2 %finish.1 = (f32[2,32]{1,0:T(2,128)}, f32[1,2]{1,0:T(1,128)}, f32[1,2]{1,0:T(1,128)}) custom-call(f32[4,128]{1,0:T(4,128)} %layer.1.result_ref), custom_call_target="tpu_custom_call" | custom-call | tf_op jit(solution)/shard_map/finish/pallas_call | solution.py:919
